TPU v7x, 512 devices: a whole 4x4x16 slice. The times are simulated.
512 devices in a mesh: blk: 32 (over x, y, z_hi), rel: 16 (over z_lo, core).
Axes of the slice: x: 4, y: 4, z: 16 (z_hi: 2, z_lo: 8; z = z_hi * 8 + z_lo), core: 2. Of those that a mesh axis runs over, the one named last changes fastest.
Arguments:
- features: bfloat16 [16384, 512], P(('blk', 'rel')), may hold values from -6 to 6
- adjacency: int32 [6, 512, 16, 1024], P(None, 'blk', 'rel'), may hold values from -2147483648 to 2147483646, as said below
- tile_mask: int32 [6, 128, 32, 16], P(None, 'blk', None, 'rel'), may hold values from 0 to 1
- bases: bfloat16 [512, 8, 512], P('rel'), may hold values from -0.25 to 0.25
- coefficients: float32 [6, 8], replicated, may hold values from -2 to 2
- self_weight: bfloat16 [512, 512], P('rel'), may hold values from -0.25 to 0.25
Outputs:
- updated: bfloat16 [16384, 512], P(('blk', 'rel'))
Inputs may be any that keep to these rules, and one draw needn't show every extreme that they name: `adjacency`: each word holds 32 edge bits, bit t for destination node 32 * word index + t.
All inputs are finite; a program needn't handle non-finite values.
Results may differ from a plain program's by a relative error of at most 0.0058.
Values may be sent and summed in bfloat16 or wider, within the bound.
A program may use at most 64 MiB of HBM per device.

v0:
```python
import jax
import jax.numpy as jnp
from jax import lax
from jax.sharding import Mesh
from jax.sharding import PartitionSpec as P

BLK = ("blk_0", "blk_1", "blk_2")
BLK_REL = ("blk_0", "blk_1", "blk_2", "rel")


def in_order(tiles, dim):
    shape = list(tiles.shape[1:])
    shape[dim] *= tiles.shape[0]
    return jnp.moveaxis(tiles, 0, dim).reshape(shape)


def gather_in_order(x, axes, turns):
    tiles = x
    for k in turns:
        tiles = lax.all_gather(tiles, axes[k])
    done = turns[::-1]
    back = [done.index(k) for k in range(len(axes))]
    tiles = tiles.transpose(*back, *range(len(axes), tiles.ndim))
    return tiles.reshape(-1, *x.shape)


def whole_of(x, axes, turns, dim):
    return in_order(gather_in_order(x, axes, turns), dim)


def split_up(x, dim, devices):
    shape = x.shape
    tiles = x.reshape(*shape[:dim], devices, shape[dim] // devices, *shape[dim + 1 :])
    return jnp.moveaxis(tiles, dim, 0)


def sum_at_owner(x, axis, dim):
    tiles = split_up(x, dim, lax.axis_size(axis))
    arrived = lax.all_to_all(tiles, axis, split_axis=0, concat_axis=0, tiled=True)
    return arrived.astype(jnp.float32).sum(axis=0)


def in_one_piece(arrays, axis, dim, along):
    columns = [a.reshape(*a.shape[:along], -1) for a in arrays]
    both = jnp.concatenate(columns, axis=along)
    whole, at, finished = (sum_at_owner(both, axis, dim), 0, [])
    for a, column in zip(arrays, columns):
        share = whole[..., at : at + column.shape[along]]
        finished.append(share.reshape(*share.shape[:along], *a.shape[along:]))
        at += column.shape[along]
    return tuple(finished)


def expand_edges(packed, tile_flags):
    shifts = jnp.arange(32, dtype=jnp.int32)
    edge_bits = jnp.bitwise_and(
        jnp.right_shift(packed[:, :, None, :], shifts[None, None, :, None]), 1
    )
    edge_bits = edge_bits.reshape(packed.shape[0], packed.shape[1] * 32, packed.shape[2])
    tile_rows = jnp.repeat(tile_flags, 128, axis=1)
    return edge_bits * tile_rows


def shards(features, adjacency, tile_mask, bases, coefficients, self_weight):
    relations = adjacency.shape[0]
    words = adjacency.shape[1]
    blocks = tile_mask.shape[2]
    sub_rows = features.shape[0]
    width = features.shape[1]
    own_rows = jnp.einsum(
        "rb,ibj->irj", coefficients, bases.astype(jnp.float32), precision=lax.Precision.HIGHEST
    ).astype(jnp.bfloat16)
    rel_weight, self_full = (
        lax.all_gather(own_rows, "rel", axis=0, tiled=True),
        lax.all_gather(self_weight, "rel", axis=0, tiled=True),
    )
    weight_all = rel_weight.reshape(width, relations * width)
    packed_all = adjacency.reshape(relations, words, blocks * sub_rows)
    flags_all = jnp.repeat(
        tile_mask.reshape(relations, tile_mask.shape[1], blocks), sub_rows, axis=2
    )
    portion = whole_of(features, BLK, (2, 0, 1), 0)
    values = jnp.dot(portion, weight_all, preferred_element_type=jnp.float32).astype(jnp.bfloat16)
    aggregate_values = values.reshape(portion.shape[0], relations, width)
    edges = expand_edges(packed_all, flags_all)
    degree = jnp.sum(edges, axis=(0, 2)).astype(jnp.float32)
    edges = edges.astype(jnp.bfloat16)
    running = jnp.einsum("rns,srd->nd", edges, aggregate_values, preferred_element_type=jnp.float32)
    message, degree = (running, degree)
    message, degree = in_one_piece(
        (message.astype(jnp.bfloat16), degree.astype(jnp.bfloat16)), "rel", 0, 1
    )
    own = jnp.dot(features, self_full, preferred_element_type=jnp.float32)
    return jax.nn.relu(own + message * lax.rsqrt(1.0 + degree)[:, None]).astype(jnp.bfloat16)


def solution(mesh):
    torus = Mesh(
        mesh.devices.reshape(4, 4, 2, mesh.shape["rel"]), ("blk_0", "blk_1", "blk_2", "rel")
    )
    placed = (
        P(BLK_REL, None),
        P(None, BLK, "rel", None),
        P(None, BLK, None, "rel"),
        P("rel", None, None),
        P(),
        P("rel", None),
    )
    return jax.shard_map(
        shards, mesh=torus, in_specs=placed, out_specs=P(BLK_REL, None), check_vma=False
    )
```

profile of v0, /device:TPU:1, one launch (start us, length us, event | category | flops | bytes accessed | tf_op | source)
XLA Modules:
  0.0 253.5 jit_solution(931051646286977591)
XLA Ops:
  6.5 16.8 %all-gather = bf16[64,512]{1,0:T(8,128)(2,1)S(1)} all-gather(bf16[32,512]{1,0:T(8,128)(2,1)} %param.6), channel_id=2, replica_groups=mesh['blk_0'=4,'blk_1'=4,'blk_2'=2,'rel'=16] {'blk_2'}, dimensions={0}, use_global_device_ids=true | all-gather | bytes 98304 | tf_op jit(solution)/shard_map/all_gather | solution.py:20
  23.3 11.4 %all-gather.1 = bf16[8,32,512]{2,1,0:T(8,128)(2,1)} all-gather(bf16[2,32,512]{2,1,0:T(8,128)(2,1)S(1)} %bitcast.54), channel_id=3, replica_groups=mesh['blk_0'=4,'blk_1'=4,'blk_2'=2,'rel'=16] {'blk_0'}, dimensions={0}, use_global_device_ids=true | all-gather | bytes 327680 | tf_op jit(solution)/shard_map/all_gather | solution.py:20
  34.8 0.0 all-gather.8.cloned.1.call-update
  34.8 0.0 all-gather.6.cloned.1.call-start
  34.8 0.0 copy-done
  34.8 1.0 fusion.3
  35.9 0.7 copy.15
  36.6 0.0 all-gather.6.cloned.1.call-update
  36.7 0.1 shift_right_arithmetic.32
  36.8 1.1 copy.23
  37.8 0.9 broadcast_in_dim.14
  38.7 0.2 reshape.48
  38.9 0.1 broadcast_in_dim.16
  39.0 0.1 broadcast_in_dim.17
  39.1 2.2 multiply_reduce_fusion
  41.4 0.2 copy.19
  41.6 5.2 %fusion = bf16[6,512,1024]{2,1,0:T(8,128)(2,1)} fusion(s32[6,4,1024]{2,1,0:T(4,128)S(1)} %reshape.48, s32[512]{0:T(512)S(1)} %shift_right_arithmetic.32, s32[6,16,1024]{2,1,0:T(8,128)S(1)} %bitcast.48), kind=kLoop, calls=%fused_computation.1 | loop fusion | flops 12582912 | bytes 6785024 | tf_op jit(solution)/shard_map/convert_element_type | solution.py:87
  46.8 21.6 %all-gather.8.cloned.1.call-done = bf16[16,2,32,512]{3,2,1,0:T(8,128)(2,1)} async-done(((bf16[4,2,32,512]{3,2,1,0:T(8,128)(2,1)}), bf16[16,2,32,512]{3,2,1,0:T(8,128)(2,1)}) %all-gather.8.cloned.1.call-update) | async-done | bytes 1048592 | tf_op jit(solution)/shard_map/all_gather | solution.py:20
  68.4 1.3 copy.17
  69.7 105.3 %all-gather.6.cloned.1.call-done = bf16[512,6,512]{2,0,1:T(8,128)(2,1)} async-done(((bf16[32,6,512]{2,0,1:T(8,128)(2,1)}), bf16[512,6,512]{2,0,1:T(8,128)(2,1)}) %all-gather.6.cloned.1.call-update) | async-done | bytes 3145744 | tf_op jit(solution)/shard_map/all_gather | solution.py:74
  175.0 4.8 %copy.16 = bf16[512,6,512]{0,2,1:T(8,128)(2,1)} copy(bf16[512,6,512]{2,0,1:T(8,128)(2,1)} %all-gather.6.cloned.1.call-done) | data formatting | bytes 6291456 | tf_op jit(solution)/shard_map/all_gather | solution.py:74
  179.8 5.7 %convolution_convert_fusion = bf16[3072,1024]{1,0:T(8,128)(2,1)S(1)} fusion(bf16[512,3072]{0,1:T(8,128)(2,1)} %bitcast.49, bf16[1024,512]{1,0:T(8,128)(2,1)S(1)} %bitcast.52), kind=kOutput, calls=%fused_computation.5 | convolution fusion | flops 3224371200 | bytes 10485760 | tf_op jit(solution)/shard_map/dot_general | solution.py:83
  185.6 0.0 copy-start.2
  185.6 0.0 copy-start.1
  185.6 3.4 %fusion.2 = bf16[512,512]{1,0:T(8,128)(2,1)S(1)} fusion(bf16[6,512,1024]{2,1,0:T(8,128)(2,1)S(1)} %bitcast.46, bf16[1024,6,512]{0,2,1:T(8,128)(2,1)S(1)} %bitcast.56), kind=kOutput, calls=%fused_computation.8 | convolution fusion | flops 3221487616 | bytes 13107200 | tf_op jit(solution)/shard_map/rns,srd->nd/dot_general | solution.py:88
  189.1 0.9 pad_maximum_fusion
  190.0 10.5 %all-to-all-start = ((bf16[16,32,513]{2,1,0:T(8,128)(2,1)}), bf16[16,32,513]{2,1,0:T(8,128)(2,1)S(1)}, u32[]{:S(2)}, u32[]{:S(2)}) async-start(bf16[16,32,513]{2,1,0:T(8,128)(2,1)} %pad_maximum_fusion), calls=%async_computation | async-start | bytes 1310720 | tf_op jit(solution)/shard_map/all_to_all | solution.py:39
  200.5 45.1 %all_gather.24 = bf16[512,512]{1,0:T(8,128)(2,1)S(1)} all-gather(bf16[32,512]{1,0:T(8,128)(2,1)S(1)} %copy-done.2), channel_id=1, replica_groups=mesh['blk_0'=4,'blk_1'=4,'blk_2'=2,'rel'=16] {'rel'}, dimensions={0}, use_global_device_ids=true | all-gather | bytes 557056 | tf_op jit(solution)/shard_map/all_gather | solution.py:75
  245.6 0.0 all-to-all-done
  245.6 0.1 convert_reduce_fusion
  245.7 0.1 fusion.7
  245.8 0.8 fusion.5
  (11 shorter events, 0.0 us)
Async XLA Ops:
  6.5 28.3 %copy-start = (bf16[32,8,512]{2,1,0:T(8,128)(2,1)S(1)}, bf16[32,8,512]{2,1,0:T(8,128)(2,1)}, u32[]{:S(2)}) copy-start(bf16[32,8,512]{2,1,0:T(8,128)(2,1)} %param.9) | copy-start | bytes 786436
  6.5 61.9 %all-gather.8.cloned.1.call-start = ((), (), s32[]{:S(2)}) async-start(), calls=%async_computation.2 | async-start | bytes 1310720 | tf_op jit(solution)/shard_map/all_gather | solution.py:20
  34.8 140.2 %all-gather.6.cloned.1.call-start = ((), (), s32[]{:S(2)}) async-start(), calls=%async_computation.1 | async-start | bytes 3342336 | tf_op jit(solution)/shard_map/all_gather | solution.py:74
  175.0 10.6 %slice-start = ((s8[6291456]{0:T(1024)(128)(4,1)}), s8[2097152]{0:T(1024)(128)(4,1)S(1)}, s32[]{:S(2)}) async-start(s8[6291456]{0:T(1024)(128)(4,1)} %bitcast.45), calls=%async_computation.3 | async-start | bytes 4194304
  179.8 5.7 %slice-start.1 = ((s8[6291456]{0:T(1024)(128)(4,1)}), s8[4194304]{0:T(1024)(128)(4,1)S(1)}, s32[]{:S(2)}) async-start(s8[6291456]{0:T(1024)(128)(4,1)} %bitcast.45), calls=%async_computation.4 | async-start | bytes 8388608
  185.6 14.8 %copy-start.2 = (bf16[32,512]{1,0:T(8,128)(2,1)S(1)}, bf16[32,512]{1,0:T(8,128)(2,1)}, u32[]{:S(2)}) copy-start(bf16[32,512]{1,0:T(8,128)(2,1)} %param.11) | copy-start | bytes 98308
  185.6 60.2 %copy-start.1 = (bf16[32,512]{1,0:T(8,128)(2,1)S(1)}, bf16[32,512]{1,0:T(8,128)(2,1)}, u32[]{:S(2)}) copy-start(bf16[32,512]{1,0:T(8,128)(2,1)} %param.6) | copy-start | bytes 98308
  190.0 55.6 %all-to-all-start = ((bf16[16,32,513]{2,1,0:T(8,128)(2,1)}), bf16[16,32,513]{2,1,0:T(8,128)(2,1)S(1)}, u32[]{:S(2)}, u32[]{:S(2)}) async-start(bf16[16,32,513]{2,1,0:T(8,128)(2,1)} %pad_maximum_fusion), calls=%async_computation | async-start | bytes 1310720 | tf_op jit(solution)/shard_map/all_to_all | solution.py:39
Sparse Core Ops, SparseCore 0:
  34.9 33.4 all-gather.7
  70.5 104.4 all-gather.5
where the time goes:
time: 254 us; the launch traced here: 253 us
  waiting for transfers between devices  127 us (50%)
  blocking collectives  73.3 us (29%)
  between operations  13.5 us (5%)
  matrix products  11 us (4%)
  starting transfers between devices  10.5 us (4%)
  local copies, waits for them, and re-layouts  9.54 us (4%)
  other arithmetic  8.61 us (3%)
    all_gather x1, waiting for transfers between devices, shards(): lax.all_gather(own_rows, 'rel', axis=0, tiled=True)  105 us
    all_gather x1, blocking collectives, shards(): lax.all_gather(self_weight, 'rel', axis=0, tiled=True)  45.1 us
    all_gather x2, blocking collectives, gather_in_order(): tiles = lax.all_gather(tiles, axes[k])  28.2 us
    all_gather x1, waiting for transfers between devices, gather_in_order(): tiles = lax.all_gather(tiles, axes[k])  21.6 us
    all_to_all x1, starting transfers between devices, sum_at_owner(): lax.all_to_all(tiles, axis, split_axis=0, concat_axis=0, tiled=True)  10.5 us
    dot_general x1, matrix products, shards(): jnp.dot(portion, weight_all, preferred_element_type=jnp.float32)  5.73 us
    convert_element_type x1, other arithmetic, shards(): edges = edges.astype(jnp.bfloat16)  5.23 us
  transfers between devices with their start and end apart: 3, of which 2 were waited for; matrix products, arithmetic and copies ran while one was open for 5% of the time, Pallas kernels for 0%

commit v1 on v0

--- a/solution.py
+++ b/solution.py
@@ -72,7 +72,9 @@
     ).astype(jnp.bfloat16)
     rel_weight, self_full = (
         lax.all_gather(own_rows, "rel", axis=0, tiled=True),
-        lax.all_gather(self_weight, "rel", axis=0, tiled=True),
+        jnp.concatenate(
+            lax.all_to_all(jnp.stack([self_weight] * lax.axis_size("rel")), "rel", 0, 0), axis=0
+        ),
     )
     weight_all = rel_weight.reshape(width, relations * width)
     packed_all = adjacency.reshape(relations, words, blocks * sub_rows)

time: 254 us -> 274 us (1.079)
  waiting for transfers between devices: 127 us -> 153 us
  starting transfers between devices: 10.5 us -> 5.23 us
    all_gather x1 -> x0, blocking collectives: 45.1 us -> none  [shards(): lax.all_gather(self_weight, 'rel', axis=0, tiled=True)]
    all_to_all x0 -> x1, blocking collectives: none -> 44.5 us  [sum_at_owner(): lax.all_to_all(tiles, axis, split_axis=0, concat_axis=0, tiled=True)]
    all_to_all x1, waiting for transfers between devices: 0.01 us -> 26 us  [shards(): lax.all_to_all(jnp.stack([self_weight] * lax.axis_size('rel')), 'rel', 0, 0)]
    all_to_all x1, starting transfers between devices: 10.5 us -> 5.19 us  [shards(): lax.all_to_all(jnp.stack([self_weight] * lax.axis_size('rel')), 'rel', 0, 0)]
  transfers between devices with their start and end apart: 3 -> 3, of which waited for: 2 -> 3; matrix products, arithmetic and copies ran while one was open for 5% -> 5% of each run, Pallas kernels for 0% -> 0%
where the time goes in v1:
time: 274 us
  waiting for transfers between devices  153 us (56%)
  blocking collectives  72.8 us (27%)
  between operations  13.5 us (5%)
  matrix products  11 us (4%)
  local copies, waits for them, and re-layouts  10.4 us (4%)
  other arithmetic  7.76 us (3%)
  starting transfers between devices  5.23 us (2%)
    all_gather x1, waiting for transfers between devices, shards(): lax.all_gather(own_rows, 'rel', axis=0, tiled=True)  105 us
    all_to_all x1, blocking collectives, sum_at_owner(): lax.all_to_all(tiles, axis, split_axis=0, concat_axis=0, tiled=True)  44.5 us
    all_gather x2, blocking collectives, gather_in_order(): tiles = lax.all_gather(tiles, axes[k])  28.2 us
    all_to_all x1, waiting for transfers between devices, shards(): lax.all_to_all(jnp.stack([self_weight] * lax.axis_size('rel')), 'rel', 0, 0)  26 us
    all_gather x1, waiting for transfers between devices, gather_in_order(): tiles = lax.all_gather(tiles, axes[k])  21.6 us
    dot_general x1, matrix products, shards(): jnp.dot(portion, weight_all, preferred_element_type=jnp.float32)  5.73 us
  transfers between devices with their start and end apart: 3, of which 3 were waited for; matrix products, arithmetic and copies ran while one was open for 5% of the time, Pallas kernels for 0%

profile of v1, /device:TPU:1, one launch (start us, length us, event | category | flops | bytes accessed | tf_op | source)
XLA Modules:
  0.0 273.6 jit_solution(2114125113564285046)
XLA Ops:
  6.5 16.8 %all-gather = bf16[64,512]{1,0:T(8,128)(2,1)S(1)} all-gather(bf16[32,512]{1,0:T(8,128)(2,1)} %param.6), channel_id=2, replica_groups=mesh['blk_0'=4,'blk_1'=4,'blk_2'=2,'rel'=16] {'blk_2'}, dimensions={0}, use_global_device_ids=true | all-gather | bytes 98304 | tf_op jit(solution)/shard_map/all_gather | solution.py:20
  23.3 11.4 %all-gather.1 = bf16[8,32,512]{2,1,0:T(8,128)(2,1)} all-gather(bf16[2,32,512]{2,1,0:T(8,128)(2,1)S(1)} %bitcast.56), channel_id=3, replica_groups=mesh['blk_0'=4,'blk_1'=4,'blk_2'=2,'rel'=16] {'blk_0'}, dimensions={0}, use_global_device_ids=true | all-gather | bytes 327680 | tf_op jit(solution)/shard_map/all_gather | solution.py:20
  34.8 0.0 all-gather.8.cloned.1.call-update
  34.8 0.0 all-gather.6.cloned.1.call-start
  34.8 1.0 fusion.3
  35.9 0.7 copy.15
  36.6 0.0 all-gather.6.cloned.1.call-update
  36.7 0.1 shift_right_arithmetic.32
  36.8 1.1 copy.23
  37.8 0.9 broadcast_in_dim.14
  38.7 0.2 reshape.54
  38.9 0.1 broadcast_in_dim.16
  39.0 0.1 broadcast_in_dim.17
  39.1 2.2 multiply_reduce_fusion
  41.4 0.2 copy.19
  41.6 5.2 %fusion = bf16[6,512,1024]{2,1,0:T(8,128)(2,1)} fusion(s32[6,4,1024]{2,1,0:T(4,128)S(1)} %reshape.54, s32[512]{0:T(512)S(1)} %shift_right_arithmetic.32, s32[6,16,1024]{2,1,0:T(8,128)S(1)} %bitcast.49), kind=kLoop, calls=%fused_computation.1 | loop fusion | flops 12582912 | bytes 6785024 | tf_op jit(solution)/shard_map/convert_element_type | solution.py:89
  46.8 21.6 %all-gather.8.cloned.1.call-done = bf16[16,2,32,512]{3,2,1,0:T(8,128)(2,1)} async-done(((bf16[4,2,32,512]{3,2,1,0:T(8,128)(2,1)}), bf16[16,2,32,512]{3,2,1,0:T(8,128)(2,1)}) %all-gather.8.cloned.1.call-update) | async-done | bytes 1048592 | tf_op jit(solution)/shard_map/all_gather | solution.py:20
  68.4 1.3 copy.17
  69.7 105.3 %all-gather.6.cloned.1.call-done = bf16[512,6,512]{2,0,1:T(8,128)(2,1)} async-done(((bf16[32,6,512]{2,0,1:T(8,128)(2,1)}), bf16[512,6,512]{2,0,1:T(8,128)(2,1)}) %all-gather.6.cloned.1.call-update) | async-done | bytes 3145744 | tf_op jit(solution)/shard_map/all_gather | solution.py:74
  175.0 4.8 %copy.16 = bf16[512,6,512]{0,2,1:T(8,128)(2,1)} copy(bf16[512,6,512]{2,0,1:T(8,128)(2,1)} %all-gather.6.cloned.1.call-done) | data formatting | bytes 6291456 | tf_op jit(solution)/shard_map/all_gather | solution.py:74
  179.8 5.7 %convolution_convert_fusion = bf16[3072,1024]{1,0:T(8,128)(2,1)S(1)} fusion(bf16[512,3072]{0,1:T(8,128)(2,1)} %bitcast.50, bf16[1024,512]{1,0:T(8,128)(2,1)S(1)} %bitcast.54), kind=kOutput, calls=%fused_computation.5 | convolution fusion | flops 3224371200 | bytes 10485760 | tf_op jit(solution)/shard_map/dot_general | solution.py:85
  185.6 0.0 copy-start.2
  185.6 0.0 copy-start.1
  185.6 3.4 %fusion.2 = bf16[512,512]{1,0:T(8,128)(2,1)S(1)} fusion(bf16[6,512,1024]{2,1,0:T(8,128)(2,1)S(1)} %bitcast.47, bf16[1024,6,512]{0,2,1:T(8,128)(2,1)S(1)} %bitcast.58), kind=kOutput, calls=%fused_computation.8 | convolution fusion | flops 3221487616 | bytes 13107200 | tf_op jit(solution)/shard_map/rns,srd->nd/dot_general | solution.py:90
  189.1 0.1 pad_maximum_fusion
  189.2 44.5 %all_to_all.10 = bf16[16,32,513]{2,1,0:T(8,128)(2,1)S(1)} all-to-all(bf16[16,32,513]{2,1,0:T(8,128)(2,1)S(1)} %pad_maximum_fusion), channel_id=1, replica_groups=mesh['blk_0'=4,'blk_1'=4,'blk_2'=2,'rel'=16] {'rel'}, dimensions={0} | all-to-all | bytes 1050624 | tf_op jit(solution)/shard_map/all_to_all | solution.py:39
  233.7 0.8 stack.2
  234.5 5.2 %all-to-all-start = ((bf16[16,32,512]{2,1,0:T(8,128)(2,1)}), bf16[16,32,512]{2,1,0:T(8,128)(2,1)S(1)}, u32[]{:S(2)}, u32[]{:S(2)}) async-start(bf16[16,32,512]{2,1,0:T(8,128)(2,1)} %stack.2), calls=%async_computation | async-start | bytes 1048576 | tf_op jit(solution)/shard_map/all_to_all | solution.py:76
  239.7 0.1 convert_reduce_fusion
  239.8 0.1 fusion.7
  239.9 26.0 %all-to-all-done = bf16[16,32,512]{2,1,0:T(8,128)(2,1)S(1)} async-done(((bf16[16,32,512]{2,1,0:T(8,128)(2,1)}), bf16[16,32,512]{2,1,0:T(8,128)(2,1)S(1)}, u32[]{:S(2)}, u32[]{:S(2)}) %all-to-all-start) | async-done | bytes 524320 | tf_op jit(solution)/shard_map/all_to_all | solution.py:76
  266.0 0.8 fusion.5
  (12 shorter events, 0.0 us)
Async XLA Ops:
  6.5 28.3 %copy-start = (bf16[32,8,512]{2,1,0:T(8,128)(2,1)S(1)}, bf16[32,8,512]{2,1,0:T(8,128)(2,1)}, u32[]{:S(2)}) copy-start(bf16[32,8,512]{2,1,0:T(8,128)(2,1)} %param.9) | copy-start | bytes 786436
  6.5 61.9 %all-gather.8.cloned.1.call-start = ((), (), s32[]{:S(2)}) async-start(), calls=%async_computation.3 | async-start | bytes 1310720 | tf_op jit(solution)/shard_map/all_gather | solution.py:20
  34.8 140.2 %all-gather.6.cloned.1.call-start = ((), (), s32[]{:S(2)}) async-start(), calls=%async_computation.2 | async-start | bytes 3342336 | tf_op jit(solution)/shard_map/all_gather | solution.py:74
  175.0 10.6 %slice-start = ((s8[6291456]{0:T(1024)(128)(4,1)}), s8[2097152]{0:T(1024)(128)(4,1)S(1)}, s32[]{:S(2)}) async-start(s8[6291456]{0:T(1024)(128)(4,1)} %bitcast.46), calls=%async_computation.4 | async-start | bytes 4194304
  179.8 5.7 %slice-start.1 = ((s8[6291456]{0:T(1024)(128)(4,1)}), s8[4194304]{0:T(1024)(128)(4,1)S(1)}, s32[]{:S(2)}) async-start(s8[6291456]{0:T(1024)(128)(4,1)} %bitcast.46), calls=%async_computation.5 | async-start | bytes 8388608
  185.6 48.1 %copy-start.2 = (bf16[32,512]{1,0:T(8,128)(2,1)S(1)}, bf16[32,512]{1,0:T(8,128)(2,1)}, u32[]{:S(2)}) copy-start(bf16[32,512]{1,0:T(8,128)(2,1)} %param.11) | copy-start | bytes 98308
  185.6 80.3 %copy-start.1 = (bf16[32,512]{1,0:T(8,128)(2,1)S(1)}, bf16[32,512]{1,0:T(8,128)(2,1)}, u32[]{:S(2)}) copy-start(bf16[32,512]{1,0:T(8,128)(2,1)} %param.6) | copy-start | bytes 98308
  234.5 31.4 %all-to-all-start = ((bf16[16,32,512]{2,1,0:T(8,128)(2,1)}), bf16[16,32,512]{2,1,0:T(8,128)(2,1)S(1)}, u32[]{:S(2)}, u32[]{:S(2)}) async-start(bf16[16,32,512]{2,1,0:T(8,128)(2,1)} %stack.2), calls=%async_computation | async-start | bytes 1048576 | tf_op jit(solution)/shard_map/all_to_all | solution.py:76
Sparse Core Ops, SparseCore 0:
  34.9 33.4 all-gather.7
  70.5 104.4 all-gather.5
